TPU v7x, 32 devices: a whole 2x2x4 slice. The times are simulated.
32 devices in a mesh: dp: 8 (over z, y), mp: 4 (over x, core).
Axes of the slice: x: 2, y: 2, z: 4, core: 2. Of those that a mesh axis runs over, the one named last changes fastest.
Arguments:
- logits: bfloat16 [1024, 16384], P('dp', 'mp'), may hold values from -72 to 240
- targets: int32 [1024], P('dp'), may hold values from 0 to 16383
- resp_mask: int32 [1024], P('dp'), may hold values from 0 to 1, as said below
- rewards: int32 [8], P('dp'), may hold values from 0 to 10
- groups: int32 [8], P('dp'), may hold values from 0 to 1, as said below
- unit_grad: bfloat16 [1024, 8192], P(('dp', 'mp')), may hold values from -192 to 192
- mix: bfloat16 [1024, 2048], P('dp', 'mp'), may hold values from -6 to 6
- w_out: bfloat16 [2048, 8192], P('mp', 'dp'), may hold values from -0.125 to 0.125
Outputs:
- token_logprob: float32 [1024], P('dp')
- policy_loss: float32 [], replicated
- grad_mix: bfloat16 [1024, 2048], P('dp', 'mp')
- grad_w_out: bfloat16 [2048, 8192], P('mp', 'dp')
Inputs may be any that keep to these rules, and one draw needn't show every extreme that they name: `resp_mask`: in each sample the response mask is a run of ones followed by zeros, with at least 32 ones. `groups`: each prompt id names exactly 4 samples.
All inputs are finite; a program needn't handle non-finite values.
Results may differ from a plain program's by a relative error of at most 0.005.
Values may be sent and summed in bfloat16 or wider, within the bound.
A program may use at most 64 MiB of HBM per device.

v0:
```python
import jax
import jax.numpy as jnp
from jax import lax
from jax.sharding import PartitionSpec as P

K = 4


def shards(logits, targets, resp_mask, rewards, groups, unit_grad, mix, w_out):
    tok_rows, vocab_dev = logits.shape
    mp_lane = lax.axis_index("mp")
    local_target = targets - mp_lane * vocab_dev
    present = (local_target >= 0) & (local_target < vocab_dev)
    picked = jnp.take_along_axis(logits, jnp.clip(local_target, 0, vocab_dev - 1)[:, None], axis=1)[
        :, 0
    ]
    picked = jnp.where(present, picked.astype(jnp.float32), 0.0)
    local_max = jnp.max(logits, axis=1).astype(jnp.float32)
    highest = lax.pmax(local_max, "mp")
    local_sum = jnp.sum(jnp.exp(logits.astype(jnp.float32) - highest[:, None]), axis=1)
    summed, target_logit = lax.psum((local_sum, picked), "mp")
    logprob = target_logit - (highest + jnp.log(summed))
    mask_float = resp_mask.astype(jnp.float32)
    local_count = jnp.sum(mask_float)
    reward_float = rewards.astype(jnp.float32)
    prompt_slots = jnp.arange(lax.axis_size("dp") // K, dtype=jnp.int32)
    own_slot = (prompt_slots == groups[0]).astype(jnp.float32)
    group_total, token_count = lax.psum((own_slot * reward_float[0], local_count), "dp")
    own_total = jnp.sum(own_slot * group_total)
    advantage = reward_float[0] - (own_total - reward_float[0]) / (K - 1)
    weight = advantage * mask_float / token_count
    policy_loss = lax.psum(-jnp.sum(weight * logprob), "dp")
    sub_rows = unit_grad.shape[0]
    part_weight = lax.dynamic_slice_in_dim(weight, mp_lane * sub_rows, sub_rows)
    grad_local = (-part_weight[:, None] * unit_grad.astype(jnp.float32)).astype(jnp.bfloat16)
    grad_group = lax.all_gather(grad_local, "mp", axis=0, tiled=True)
    grad_mix = lax.dot_general(
        grad_group,
        lax.all_gather(w_out, "dp", axis=1, tiled=True),
        (((1,), (1,)), ((), ())),
        preferred_element_type=jnp.float32,
    ).astype(jnp.bfloat16)
    grad_every = lax.all_to_all(grad_group, "dp", split_axis=1, concat_axis=0, tiled=True)
    grad_w_out = lax.dot_general(
        lax.all_gather(mix, "dp", axis=0, tiled=True),
        grad_every,
        (((0,), (0,)), ((), ())),
        preferred_element_type=jnp.float32,
    ).astype(jnp.bfloat16)
    return (logprob, policy_loss, grad_mix, grad_w_out)


def solution(mesh):
    return jax.shard_map(
        shards,
        mesh=mesh,
        in_specs=(
            P("dp", "mp"),
            P("dp"),
            P("dp"),
            P("dp"),
            P("dp"),
            P(("dp", "mp"), None),
            P("dp", "mp"),
            P("mp", "dp"),
        ),
        out_specs=(P("dp"), P(), P("dp", "mp"), P("mp", "dp")),
        check_vma=False,
    )
```

profile of v0, /device:TPU:0, one launch (start us, length us, event | category | flops | bytes accessed | tf_op | source)
XLA Modules:
  0.0 279.9 jit_solution(4905215738061434298)
XLA Ops:
  7.2 0.0 copy-start.2
  7.2 0.0 copy-start.1
  7.2 0.0 all-gather.4.cloned.1.call-start
  7.2 1.3 convert_reduce_fusion
  9.9 23.8 %all-reduce = (f32[]{:T(128)}, f32[2]{0:T(128)S(1)}) all-reduce(f32[]{:T(128)} %convert_reduce_fusion, f32[2]{0:T(128)S(1)} %compare_select_fusion.2), channel_id=1, replica_groups=mesh['dp'=8,'mp'=4] {'dp'}, use_global_device_ids=true, to_apply=%region_8.9 | all-reduce | flops 3 | bytes 24 | tf_op jit(solution)/shard_map/psum | solution.py:28
  33.6 0.6 fusion.1
  34.9 0.7 fusion.2
  35.6 2.3 gather_fusion
  37.9 0.7 and_select_fusion.1
  38.5 1.4 reduce_max.9
  40.0 5.7 %pmax.7 = f32[128]{0:T(128)S(1)} all-reduce(bf16[128]{0:T(256)(128)(2,1)S(1)} %reduce_max.9), channel_id=1, replica_groups=mesh['dp'=8,'mp'=4] {'mp'}, use_global_device_ids=true, to_apply=%region_2.3 | all-reduce | flops 128 | bytes 768 | tf_op jit(solution)/shard_map/pmax | solution.py:19
  45.6 1.7 exponential_reduce_fusion
  47.4 6.6 %all-reduce.1 = (f32[128]{0:T(128)S(1)}, f32[128]{0:T(128)S(1)}) all-reduce(f32[128]{0:T(128)S(1)} %and_select_fusion.1, f32[128]{0:T(128)S(1)} %exponential_reduce_fusion), channel_id=1, replica_groups=mesh['dp'=8,'mp'=4] {'mp'}, use_global_device_ids=true, to_apply=%region_0.1 | all-reduce | flops 256 | bytes 2048 | tf_op jit(solution)/shard_map/psum | solution.py:21
  53.9 0.0 copy-done.2
  53.9 1.8 multiply_reduce_fusion
  55.7 0.1 dynamic-slice_negate_fusion
  55.8 0.0 copy-done.1
  55.8 0.9 multiply_convert_fusion
  56.7 0.0 all-gather.4.cloned.1.call-update
  56.7 0.0 all-gather.8.cloned.1.call-start
  56.8 0.7 all-gather.8.cloned.1.call-update
  57.5 0.0 all-gather.6.cloned.1.call-start
  57.5 0.7 all-gather.6.cloned.1.call-update
  58.2 18.0 %all-gather.4.cloned.1.call-done = bf16[128,8192]{1,0:T(8,128)(2,1)} async-done(((bf16[32,8192]{1,0:T(8,128)(2,1)}), bf16[128,8192]{1,0:T(8,128)(2,1)}) %all-gather.4.cloned.1.call-update) | async-done | bytes 2097168 | tf_op jit(solution)/shard_map/all_gather | solution.py:36
  76.2 4.1 %copy.17 = bf16[128,8192]{0,1:T(8,128)(2,1)} copy(bf16[128,8192]{1,0:T(8,128)(2,1)} %all-gather.4.cloned.1.call-done) | data formatting | bytes 4194304 | tf_op jit(solution)/shard_map/all_gather | solution.py:36
  80.3 5.5 %all-to-all-start = ((bf16[128,8,1024]{0,2,1:T(8,128)(2,1)}), bf16[128,8,1024]{0,2,1:T(8,128)(2,1)S(1)}, u32[]{:S(2)}, u32[]{:S(2)}) async-start(bf16[128,8,1024]{0,2,1:T(8,128)(2,1)} %bitcast.20), calls=%async_computation | async-start | bytes 4194304 | tf_op jit(solution)/shard_map/all_to_all | solution.py:43
  86.4 56.0 %psum.39 = f32[]{:T(128)} all-reduce(f32[]{:T(128)S(6)} %neg.7), channel_id=1, replica_groups=mesh['dp'=8,'mp'=4] {'dp'}, use_global_device_ids=true, to_apply=%region_10.11 | all-reduce | flops 1 | bytes 8 | tf_op jit(solution)/shard_map/psum | solution.py:32
  142.5 4.6 %all-to-all-done = bf16[128,8,1024]{0,2,1:T(8,128)(2,1)S(1)} async-done(((bf16[128,8,1024]{0,2,1:T(8,128)(2,1)}), bf16[128,8,1024]{0,2,1:T(8,128)(2,1)S(1)}, u32[]{:S(2)}, u32[]{:S(2)}) %all-to-all-start) | async-done | bytes 2097184 | tf_op jit(solution)/shard_map/all_to_all | solution.py:43
  147.1 2.6 copy.18
  149.7 0.0 all-gather.8.cloned.1.call-done
  149.7 3.4 %fusion = bf16[512,1024]{0,1:T(8,128)(2,1)S(1)} fusion(bf16[1024,1024]{1,0:T(8,128)(2,1)} %bitcast.21, bf16[1024,512]{1,0:T(8,128)(2,1)} %all-gather.8.cloned.1.call-done), kind=kOutput, calls=%fused_computation.3 | convolution fusion | flops 1074266112 | bytes 4194304 | tf_op jit(solution)/shard_map/dot_general | solution.py:44
  153.1 0.0 copy-start
  153.1 1.3 copy.19
  154.4 112.0 %all-gather.6.cloned.1.call-done = bf16[512,8192]{1,0:T(8,128)(2,1)} async-done(((bf16[512,1024]{1,0:T(8,128)(2,1)}), bf16[512,8192]{1,0:T(8,128)(2,1)}) %all-gather.6.cloned.1.call-update) | async-done | bytes 8388624 | tf_op jit(solution)/shard_map/all_gather | solution.py:39
  266.4 0.0 copy-done
  266.4 7.0 %convolution_convert_fusion.1 = bf16[128,512]{1,0:T(8,128)(2,1)} fusion(bf16[128,8192]{1,0:T(8,128)(2,1)S(1)} %copy-done, bf16[512,8192]{1,0:T(8,128)(2,1)} %all-gather.6.cloned.1.call-done), kind=kOutput, calls=%fused_computation.4 | convolution fusion | flops 1073807360 | bytes 10616832 | tf_op jit(solution)/shard_map/dot_general | solution.py:37
  (4 shorter events, 0.0 us)
Async XLA Ops:
  7.2 46.8 %copy-start.2 = (s32[128]{0:T(128)S(1)}, s32[128]{0:T(128)}, u32[]{:S(2)}) copy-start(s32[128]{0:T(128)} %param.10) | copy-start | bytes 1540
  7.2 48.6 %copy-start.1 = (bf16[32,8192]{1,0:T(8,128)(2,1)S(1)}, bf16[32,8192]{1,0:T(8,128)(2,1)}, u32[]{:S(2)}) copy-start(bf16[32,8192]{1,0:T(8,128)(2,1)} %param.13) | copy-start | bytes 1572868
  7.2 69.0 %all-gather.4.cloned.1.call-start = ((), (), s32[]{:S(2)}) async-start(), calls=%async_computation.1 | async-start | bytes 2621440 | tf_op jit(solution)/shard_map/all_gather | solution.py:36
  56.7 92.9 %all-gather.8.cloned.1.call-start = ((), (), s32[]{:S(2)}) async-start(), calls=%async_computation.3 | async-start | bytes 1179648 | tf_op jit(solution)/shard_map/all_gather | solution.py:45
  57.5 208.9 %all-gather.6.cloned.1.call-start = ((), (), s32[]{:S(2)}) async-start(), calls=%async_computation.2 | async-start | bytes 9437184 | tf_op jit(solution)/shard_map/all_gather | solution.py:39
  80.3 66.8 %all-to-all-start = ((bf16[128,8,1024]{0,2,1:T(8,128)(2,1)}), bf16[128,8,1024]{0,2,1:T(8,128)(2,1)S(1)}, u32[]{:S(2)}, u32[]{:S(2)}) async-start(bf16[128,8,1024]{0,2,1:T(8,128)(2,1)} %bitcast.20), calls=%async_computation | async-start | bytes 4194304 | tf_op jit(solution)/shard_map/all_to_all | solution.py:43
  153.1 113.3 %copy-start = (bf16[128,8192]{1,0:T(8,128)(2,1)S(1)}, bf16[128,8192]{1,0:T(8,128)(2,1)}, u32[]{:S(2)}) copy-start(bf16[128,8192]{1,0:T(8,128)(2,1)} %all-gather.4.cloned.1.call-done) | copy-start | bytes 6291460
Sparse Core Ops, SparseCore 0:
  56.9 19.2 all-gather.3
  78.3 63.1 all-gather.7
  143.7 122.6 all-gather.5
where the time goes:
time: 280 us
  waiting for transfers between devices  136 us (49%)
  blocking collectives  92 us (33%)
  between operations  16.4 us (6%)
  matrix products  10.4 us (4%)
  local copies, waits for them, and re-layouts  10.3 us (4%)
  other arithmetic  9.22 us (3%)
  starting transfers between devices  5.63 us (2%)
    all_gather x1, waiting for transfers between devices, shards(): lax.all_gather(w_out, 'dp', axis=1, tiled=True)  112 us
    psum x1, blocking collectives, shards(): policy_loss = lax.psum(-jnp.sum(weight * logprob), 'dp')  56 us
    psum x1, blocking collectives, shards(): lax.psum((own_slot * reward_float[0], local_count), 'dp')  23.8 us
    all_gather x1, waiting for transfers between devices, shards(): grad_group = lax.all_gather(grad_local, 'mp', axis=0, tiled=True)  18 us
    dot_general x1, matrix products, shards(): lax.dot_general(grad_group, lax.all_gather(w_out, 'dp', axis=1, tiled=Tru...  6.96 us
    psum x1, blocking collectives, shards(): summed, target_logit = lax.psum((local_sum, picked), 'mp')  6.56 us
    pmax x1, blocking collectives, shards(): highest = lax.pmax(local_max, 'mp')  5.66 us
  transfers between devices with their start and end apart: 4, of which 3 were waited for; matrix products, arithmetic and copies ran while one was open for 4% of the time, Pallas kernels for 0%

commit v1 on v0

--- a/solution.py
+++ b/solution.py
@@ -33,7 +33,12 @@
     sub_rows = unit_grad.shape[0]
     part_weight = lax.dynamic_slice_in_dim(weight, mp_lane * sub_rows, sub_rows)
     grad_local = (-part_weight[:, None] * unit_grad.astype(jnp.float32)).astype(jnp.bfloat16)
-    grad_group = lax.all_gather(grad_local, "mp", axis=0, tiled=True)
+    ring = [grad_local]
+    for hop in range(3):
+        ring.append(lax.ppermute(ring[-1], "mp", [(dev, (dev + 1) % 4) for dev in range(4)]))
+    grad_group = jnp.roll(
+        jnp.concatenate(ring[::-1], axis=0), (lax.axis_index("mp") + 1) * ring[0].shape[0], axis=0
+    )
     grad_mix = lax.dot_general(
         grad_group,
         lax.all_gather(w_out, "dp", axis=1, tiled=True),

time: 280 us -> 240 us (0.86)
  waiting for transfers between devices: 136 us -> 83.4 us
  blocking collectives: 92 us -> 104 us
    all_gather x1, waiting for transfers between devices: 112 us -> 26.4 us  [shards(): lax.all_gather(w_out, 'dp', axis=1, tiled=True)]
    all_to_all x1, waiting for transfers between devices: 4.61 us -> 30.5 us  [shards(): lax.all_to_all(grad_group, 'dp', split_axis=1, concat_axis=0, tiled=True)]
    ppermute x0 -> x3, waiting for transfers between devices: none -> 25.8 us  [shards(): lax.ppermute(ring[-1], 'mp', [(dev, (dev + 1) % 4) for dev in range(4)])]
    all_gather x1 -> x0, waiting for transfers between devices: 18 us -> none  [shards(): grad_group = lax.all_gather(grad_local, 'mp', axis=0, tiled=True)]
    psum x1, blocking collectives: 56 us -> 67.1 us  [shards(): policy_loss = lax.psum(-jnp.sum(weight * logprob), 'dp')]
    all_gather x1 -> x0, local copies, waits for them, and re-layouts: 4.07 us -> none  [shards(): grad_group = lax.all_gather(grad_local, 'mp', axis=0, tiled=True)]
  transfers between devices with their start and end apart: 4 -> 6, of which waited for: 3 -> 5; matrix products, arithmetic and copies ran while one was open for 4% -> 10% of each run, Pallas kernels for 0% -> 0%
where the time goes in v1:
time: 240 us; the launch traced here: 239 us
  blocking collectives  104 us (43%)
  waiting for transfers between devices  83.4 us (35%)
  between operations  16.8 us (7%)
  local copies, waits for them, and re-layouts  10.4 us (4%)
  other arithmetic  10.4 us (4%)
  matrix products  10.2 us (4%)
  starting transfers between devices  4.49 us (2%)
    psum x1, blocking collectives, shards(): policy_loss = lax.psum(-jnp.sum(weight * logprob), 'dp')  67.1 us
    all_to_all x1, waiting for transfers between devices, shards(): lax.all_to_all(grad_group, 'dp', split_axis=1, concat_axis=0, tiled=True)  30.5 us
    all_gather x1, waiting for transfers between devices, shards(): lax.all_gather(w_out, 'dp', axis=1, tiled=True)  26.4 us
    ppermute x3, waiting for transfers between devices, shards(): lax.ppermute(ring[-1], 'mp', [(dev, (dev + 1) % 4) for dev in range(4)])  25.8 us
    psum x1, blocking collectives, shards(): lax.psum((own_slot * reward_float[0], local_count), 'dp')  23.9 us
    dot_general x1, matrix products, shards(): lax.dot_general(grad_group, lax.all_gather(w_out, 'dp', axis=1, tiled=Tru...  6.96 us
    psum x1, blocking collectives, shards(): summed, target_logit = lax.psum((local_sum, picked), 'mp')  6.67 us
    pmax x1, blocking collectives, shards(): highest = lax.pmax(local_max, 'mp')  6.06 us
  transfers between devices with their start and end apart: 6, of which 5 were waited for; matrix products, arithmetic and copies ran while one was open for 10% of the time, Pallas kernels for 0%

profile of v1, /device:TPU:0, one launch (start us, length us, event | category | flops | bytes accessed | tf_op | source)
XLA Modules:
  0.0 239.4 jit_solution(13465192785727842736)
XLA Ops:
  7.2 0.0 copy-start
  7.2 0.0 all-gather.5.cloned.1.call-start
  7.2 0.7 all-gather.5.cloned.1.call-update
  7.9 0.0 all-gather.3.cloned.1.call-start
  8.0 1.3 convert_reduce_fusion
  10.5 23.9 %all-reduce = (f32[]{:T(128)}, f32[2]{0:T(128)S(1)}) all-reduce(f32[]{:T(128)} %convert_reduce_fusion, f32[2]{0:T(128)S(1)} %compare_select_fusion.2), channel_id=1, replica_groups=mesh['dp'=8,'mp'=4] {'dp'}, use_global_device_ids=true, to_apply=%region_8.9 | all-reduce | flops 3 | bytes 24 | tf_op jit(solution)/shard_map/psum | solution.py:28
  34.4 0.6 fusion.1
  35.7 0.7 fusion.2
  36.4 2.3 gather_fusion
  38.7 0.7 and_select_fusion.1
  39.3 1.4 reduce_max.9
  40.8 6.1 %pmax.7 = f32[128]{0:T(128)S(1)} all-reduce(bf16[128]{0:T(256)(128)(2,1)S(1)} %reduce_max.9), channel_id=1, replica_groups=mesh['dp'=8,'mp'=4] {'mp'}, use_global_device_ids=true, to_apply=%region_2.3 | all-reduce | flops 128 | bytes 768 | tf_op jit(solution)/shard_map/pmax | solution.py:19
  46.9 1.7 exponential_reduce_fusion
  48.6 6.7 %all-reduce.1 = (f32[128]{0:T(128)S(1)}, f32[128]{0:T(128)S(1)}) all-reduce(f32[128]{0:T(128)S(1)} %and_select_fusion.1, f32[128]{0:T(128)S(1)} %exponential_reduce_fusion), channel_id=1, replica_groups=mesh['dp'=8,'mp'=4] {'mp'}, use_global_device_ids=true, to_apply=%region_0.1 | all-reduce | flops 256 | bytes 2048 | tf_op jit(solution)/shard_map/psum | solution.py:21
  55.3 2.4 %multiply_reduce_fusion = (f32[]{:T(128)}, f32[128]{0:T(128)S(1)}, f32[128]{0:T(128)}) fusion(f32[]{:T(128)} %get-tuple-element.24, s32[128]{0:T(128)} %param.10, f32[]{:T(128)S(6)} %sub.33, f32[128]{0:T(128)S(1)} %get-tuple-element.26, f32[128]{0:T(128)S(1)} %pmax.7, f32[128]{0:T(128)S(1)} %get-tuple-element.27), kind=kLoop, calls=%fused_computation.23 | loop fusion | flops 895 | bytes 3084 | tf_op jit(solution)/shard_map/reduce_sum | solution.py:32
  57.7 0.1 dynamic-slice_negate_fusion
  57.7 1.2 multiply_convert_fusion
  58.9 0.1 collective-permute-start
  59.0 8.6 %collective-permute-done = bf16[32,8192]{1,0:T(8,128)(2,1)S(1)} collective-permute-done((bf16[32,8192]{1,0:T(8,128)(2,1)S(1)}, bf16[32,8192]{1,0:T(8,128)(2,1)S(1)}, u32[]{:S(2)}, u32[]{:S(2)}) %collective-permute-start) | collective-permute-done | bytes 524320 | tf_op jit(solution)/shard_map/ppermute | solution.py:38
  67.6 0.0 collective-permute-start.1
  67.6 0.0 all-gather.3.cloned.1.call-update
  67.6 8.6 %collective-permute-done.1 = bf16[32,8192]{1,0:T(8,128)(2,1)S(1)} collective-permute-done((bf16[32,8192]{1,0:T(8,128)(2,1)S(1)}, bf16[32,8192]{1,0:T(8,128)(2,1)S(1)}, u32[]{:S(2)}, u32[]{:S(2)}) %collective-permute-start.1) | collective-permute-done | bytes 524320 | tf_op jit(solution)/shard_map/ppermute | solution.py:38
  76.2 0.0 collective-permute-start.2
  76.2 8.6 %collective-permute-done.2 = bf16[32,8192]{1,0:T(8,128)(2,1)S(1)} collective-permute-done((bf16[32,8192]{1,0:T(8,128)(2,1)S(1)}, bf16[32,8192]{1,0:T(8,128)(2,1)S(1)}, u32[]{:S(2)}, u32[]{:S(2)}) %collective-permute-start.2) | collective-permute-done | bytes 524320 | tf_op jit(solution)/shard_map/ppermute | solution.py:38
  84.9 0.0 copy-done
  85.0 0.2 constant_dynamic-update-slice_fusion.4
  85.2 0.2 constant_dynamic-update-slice_fusion
  85.4 0.2 constant_dynamic-slice_fusion
  85.6 2.5 %copy.27 = bf16[128,8192]{0,1:T(8,128)(2,1)} copy(bf16[128,8192]{1,0:T(8,128)(2,1)S(1)} %constant_dynamic-slice_fusion) | data formatting | bytes 4194304 | tf_op jit(solution)/shard_map/jit(_roll_dynamic)/dynamic_slice | solution.py:39
  88.0 4.4 %all-to-all-start = ((bf16[128,8,1024]{0,2,1:T(8,128)(2,1)}), bf16[128,8,1024]{0,2,1:T(8,128)(2,1)}, u32[]{:S(2)}, u32[]{:S(2)}) async-start(bf16[128,8,1024]{0,2,1:T(8,128)(2,1)} %bitcast.19), calls=%async_computation | async-start | bytes 4194304 | tf_op jit(solution)/shard_map/all_to_all | solution.py:48
  93.0 67.1 %psum.39 = f32[]{:T(128)} all-reduce(f32[]{:T(128)S(6)} %neg.7), channel_id=1, replica_groups=mesh['dp'=8,'mp'=4] {'dp'}, use_global_device_ids=true, to_apply=%region_10.11 | all-reduce | flops 1 | bytes 8 | tf_op jit(solution)/shard_map/psum | solution.py:32
  160.2 30.5 %all-to-all-done = bf16[128,8,1024]{0,2,1:T(8,128)(2,1)} async-done(((bf16[128,8,1024]{0,2,1:T(8,128)(2,1)}), bf16[128,8,1024]{0,2,1:T(8,128)(2,1)}, u32[]{:S(2)}, u32[]{:S(2)}) %all-to-all-start) | async-done | bytes 2097184 | tf_op jit(solution)/shard_map/all_to_all | solution.py:48
  190.7 3.9 %copy.28 = bf16[8,128,1024]{2,1,0:T(8,128)(2,1)} copy(bf16[8,128,1024]{1,2,0:T(8,128)(2,1)} %bitcast.6) | data formatting | bytes 4194304 | tf_op jit(solution)/shard_map/all_to_all | solution.py:48
  194.6 0.0 all-gather.5.cloned.1.call-done
  194.7 3.2 %fusion = bf16[512,1024]{0,1:T(8,128)(2,1)S(1)} fusion(bf16[1024,1024]{1,0:T(8,128)(2,1)} %bitcast.20, bf16[1024,512]{1,0:T(8,128)(2,1)} %all-gather.5.cloned.1.call-done), kind=kOutput, calls=%fused_computation.3 | convolution fusion | flops 1074266112 | bytes 4194304 | tf_op jit(solution)/shard_map/dot_general | solution.py:49
  197.9 1.3 copy.29
  199.2 26.4 %all-gather.3.cloned.1.call-done = bf16[512,8192]{1,0:T(8,128)(2,1)} async-done(((bf16[512,1024]{1,0:T(8,128)(2,1)}), bf16[512,8192]{1,0:T(8,128)(2,1)}) %all-gather.3.cloned.1.call-update) | async-done | bytes 8388624 | tf_op jit(solution)/shard_map/all_gather | solution.py:44
  225.6 7.0 %convolution_convert_fusion.1 = bf16[128,512]{1,0:T(8,128)(2,1)} fusion(bf16[128,8192]{1,0:T(8,128)(2,1)S(1)} %constant_dynamic-slice_fusion, bf16[512,8192]{1,0:T(8,128)(2,1)} %all-gather.3.cloned.1.call-done), kind=kOutput, calls=%fused_computation.4 | convolution fusion | flops 1073807360 | bytes 10616832 | tf_op jit(solution)/shard_map/dot_general | solution.py:42
  (10 shorter events, 0.2 us)
Async XLA Ops:
  7.2 77.8 %copy-start = (bf16[32,8192]{1,0:T(8,128)(2,1)S(1)}, bf16[32,8192]{1,0:T(8,128)(2,1)}, u32[]{:S(2)}) copy-start(bf16[32,8192]{1,0:T(8,128)(2,1)} %param.13) | copy-start | bytes 1572868
  7.2 187.5 %all-gather.5.cloned.1.call-start = ((), (), s32[]{:S(2)}) async-start(), calls=%async_computation.2 | async-start | bytes 1179648 | tf_op jit(solution)/shard_map/all_gather | solution.py:50
  7.9 217.7 %all-gather.3.cloned.1.call-start = ((), (), s32[]{:S(2)}) async-start(), calls=%async_computation.1 | async-start | bytes 9437184 | tf_op jit(solution)/shard_map/all_gather | solution.py:44
  58.9 8.7 %collective-permute-start = (bf16[32,8192]{1,0:T(8,128)(2,1)S(1)}, bf16[32,8192]{1,0:T(8,128)(2,1)S(1)}, u32[]{:S(2)}, u32[]{:S(2)}) collective-permute-start(bf16[32,8192]{1,0:T(8,128)(2,1)S(1)} %multiply_convert_fusion), channel_id=1, source_target_pairs={{0,1},{1,2},{2,3},{3,0},{4,5},{5,6},{6,7},{7,4},{8,9},{9,10},{10,1... | collective-permute-start | bytes 1572872 | tf_op jit(solution)/shard_map/ppermute | solution.py:38
  67.6 8.6 %collective-permute-start.1 = (bf16[32,8192]{1,0:T(8,128)(2,1)S(1)}, bf16[32,8192]{1,0:T(8,128)(2,1)S(1)}, u32[]{:S(2)}, u32[]{:S(2)}) collective-permute-start(bf16[32,8192]{1,0:T(8,128)(2,1)S(1)} %collective-permute-done), channel_id=1, source_target_pairs={{0,1},{1,2},{2,3},{3,0},{4,5},{5,6},{6,7},{7,4},{8,9},{9,10},{10,1... | collective-permute-start | bytes 1572872 | tf_op jit(solution)/shard_map/ppermute | solution.py:38
  76.2 8.6 %collective-permute-start.2 = (bf16[32,8192]{1,0:T(8,128)(2,1)S(1)}, bf16[32,8192]{1,0:T(8,128)(2,1)S(1)}, u32[]{:S(2)}, u32[]{:S(2)}) collective-permute-start(bf16[32,8192]{1,0:T(8,128)(2,1)S(1)} %collective-permute-done.1), channel_id=1, source_target_pairs={{0,1},{1,2},{2,3},{3,0},{4,5},{5,6},{6,7},{7,4},{8,9},{9,10},{10,1... | collective-permute-start | bytes 1572872 | tf_op jit(solution)/shard_map/ppermute | solution.py:38
  88.0 102.7 %all-to-all-start = ((bf16[128,8,1024]{0,2,1:T(8,128)(2,1)}), bf16[128,8,1024]{0,2,1:T(8,128)(2,1)}, u32[]{:S(2)}, u32[]{:S(2)}) async-start(bf16[128,8,1024]{0,2,1:T(8,128)(2,1)} %bitcast.19), calls=%async_computation | async-start | bytes 4194304 | tf_op jit(solution)/shard_map/all_to_all | solution.py:48
Sparse Core Ops, SparseCore 0:
  10.1 43.0 all-gather.4
  67.7 157.7 all-gather.2
